TPU v7x, 32 devices: a whole 2x2x4 slice. The times are simulated.
32 devices in a mesh: depth: 8 (over z, core), tile: 4 (over y, x).
Axes of the slice: x: 2, y: 2, z: 4, core: 2. Of those that a mesh axis runs over, the one named last changes fastest.
Arguments:
- potential: float32 [8, 1024, 384], P('depth', 'tile'), may hold values from 0 to 3
- probe: bfloat16 [2, 256, 256], replicated, may hold values from -6 to 6
- positions: int32 [4, 19, 2], P('tile'), may hold values from 0 to 128
- intensity: bfloat16 [4, 4, 256, 256], P('tile'), may hold values from 0.099609375 to 3
- fwd_wave: float32 [8, 4, 2, 256, 256], P('depth', 'tile'), may hold values from -6 to 6
- adj_wave: bfloat16 [8, 4, 2, 256, 256], P('depth', 'tile'), may hold values from -6 to 6
- saved_wave: bfloat16 [8, 4, 4, 2, 256, 256], P('depth', 'tile'), may hold values from -6 to 6
Outputs:
- fwd_next: float32 [8, 4, 2, 256, 256], P('depth', 'tile')
- adj_next: bfloat16 [8, 4, 2, 256, 256], P('depth', 'tile')
- gradient: float32 [8, 1024, 384], P('depth', 'tile')
Inputs may be any that keep to these rules, and one draw needn't show every extreme that they name: `positions`: window corners keep the whole window inside the tile's extent.
All inputs are finite; a program needn't handle non-finite values.
Results may differ from a plain program's by a relative error of at most 0.04.
Values may be sent and summed in bfloat16 or wider, within the bound.
A program may use at most 64 MiB of HBM per device.

v0:
```python
import math

import jax
import jax.numpy as jnp
from jax import lax
from jax.sharding import PartitionSpec as P

TICKS = 4


SIGMA = 0.8
DEFOCUS = 6.0


def shifted(block, axis, distance):
    devices = range(lax.axis_size(axis))
    route = [(i - distance, i) for i in devices if i - distance in devices]
    return lax.ppermute(block, axis, route)


def with_halo(block, sides, width):
    for axis, dim in sides:
        count = lax.axis_size(axis)
        forward = [(i, i + 1) for i in range(count - 1)]
        backward = [(target, source) for source, target in forward]
        low = lax.ppermute(
            lax.slice_in_dim(block, block.shape[dim] - width, None, axis=dim), axis, forward
        )
        high = lax.ppermute(lax.slice_in_dim(block, 0, width, axis=dim), axis, backward)
        block = jnp.concatenate([low, block, high], axis=dim)
    return block


def tables(n):
    idx = jnp.arange(n, dtype=jnp.int32)
    prod = idx[:, None] * idx[None, :] % n
    angle = prod.astype(jnp.float32) * (2.0 * math.pi / n)
    scale = 1.0 / math.sqrt(n)
    cos_t = (jnp.cos(angle) * scale).astype(jnp.bfloat16)
    sin_t = (jnp.sin(angle) * scale).astype(jnp.bfloat16)
    return (jnp.concatenate([cos_t, sin_t], 0), jnp.concatenate([cos_t, sin_t], 1))


def propagator(n):
    idx = jnp.arange(n, dtype=jnp.int32)
    freq = jnp.where(idx < n // 2, idx, idx - n).astype(jnp.float32)
    square = freq[:, None] * freq[:, None] + freq[None, :] * freq[None, :]
    phase = -math.pi * DEFOCUS * square / (n * n)
    return (jnp.cos(phase), jnp.sin(phase))


def left_sums(real, imag, tall_cols):
    left_r = jnp.dot(tall_cols, real.astype(jnp.bfloat16), preferred_element_type=jnp.float32)
    left_i = jnp.dot(tall_cols, imag.astype(jnp.bfloat16), preferred_element_type=jnp.float32)
    return (left_r, left_i)


def finish_left(left_r, left_i, sign, n):
    first_r = (left_r[:n] + sign * left_i[n:]).astype(jnp.bfloat16)
    first_i = (left_i[:n] - sign * left_r[n:]).astype(jnp.bfloat16)
    return (first_r, first_i)


def right_rows(first_r, first_i, broad, sign, n):
    right_r = jnp.dot(first_r, broad, preferred_element_type=jnp.float32)
    right_i = jnp.dot(first_i, broad, preferred_element_type=jnp.float32)
    return (right_r[:, :n] + sign * right_i[:, n:], right_i[:, :n] - sign * right_r[:, n:])


def forward_middle(left_r, left_i, intens, is_last, tall, broad, prop_r, prop_i, n):
    first_r, first_i = finish_left(left_r, left_i, 1.0, n)
    big_r, big_i = right_rows(first_r, first_i, broad, 1.0, n)
    far_r = big_r * prop_r - big_i * prop_i
    far_i = big_r * prop_i + big_i * prop_r
    excess = far_r * far_r + far_i * far_i - intens.astype(jnp.float32)
    src_r = jnp.where(is_last, excess * far_r, far_r)
    src_i = jnp.where(is_last, excess * far_i, far_i)
    sums_r, sums_i = left_sums(src_r, src_i, tall)
    return finish_left(sums_r, sums_i, -1.0, n)


def backward_middle(left_r, left_i, tall, broad, prop_r, prop_i, n):
    first_r, first_i = finish_left(left_r, left_i, 1.0, n)
    lr, li = right_rows(first_r, first_i, broad, 1.0, n)
    mr = lr * prop_r + li * prop_i
    mi = li * prop_r - lr * prop_i
    sums_r, sums_i = left_sums(mr, mi, tall)
    return finish_left(sums_r, sums_i, -1.0, n)


def backward_rows(first_r, first_i, saved, window, broad, n):
    lur, lui = right_rows(first_r, first_i, broad, -1.0, n)
    trans_r = jnp.cos(SIGMA * window)
    trans_i = jnp.sin(SIGMA * window)
    saved_r = saved[0].astype(jnp.float32)
    saved_i = saved[1].astype(jnp.float32)
    uar = trans_r * saved_r - trans_i * saved_i
    uai = trans_r * saved_i + trans_i * saved_r
    delta = SIGMA * (lui * uar - lur * uai)
    back = jnp.stack([trans_r * lur + trans_i * lui, trans_r * lui - trans_i * lur])
    return (back, delta)


def transmitted(window, wave):
    trans_r = jnp.cos(SIGMA * window)
    trans_i = jnp.sin(SIGMA * window)
    return (trans_r * wave[0] - trans_i * wave[1], trans_r * wave[1] + trans_i * wave[0])


def place(grad, delta, corner):
    size = delta.shape[0]
    old = lax.dynamic_slice(grad, (corner[0], corner[1]), (size, size))
    return lax.dynamic_update_slice(grad, old + delta, (corner[0], corner[1]))


def fold_final(grad, core, margin):
    inner = grad[margin : margin + core]
    from_left = shifted(grad[margin + core :].astype(jnp.bfloat16), "tile", 1).astype(jnp.float32)
    from_right = shifted(grad[:margin].astype(jnp.bfloat16), "tile", -1).astype(jnp.float32)
    inner = inner + jnp.pad(from_left, ((0, core - margin), (0, 0)))
    return inner + jnp.pad(from_right, ((core - margin, 0), (0, 0)))


def on_device(potential, probe, positions, intensity, fwd_wave, adj_wave, saved_wave):
    n = probe.shape[1]
    core = potential.shape[1]
    extent_cols = potential.shape[2]
    margin = (extent_cols - core) // 2
    sections = lax.axis_size("depth")
    section = lax.axis_index("depth")
    is_last = section == sections - 1
    is_first = section == 0
    extent = with_halo(potential[0].astype(jnp.bfloat16), (("tile", 0),), margin).astype(
        jnp.float32
    )
    tall, broad = tables(n)
    prop_r, prop_i = propagator(n)
    probe_wave = probe.astype(jnp.float32)
    wave = fwd_wave[0, 0]
    adjoint = adj_wave[0, 0]
    spots = positions[0]
    total = jnp.zeros(extent.shape, jnp.float32)
    blocks = 1
    rows = n // blocks
    f_pos = lax.dynamic_slice(spots, (2 * sections - 1 - section, 0), (1, 2))[0]
    f_win = lax.dynamic_slice(extent, (f_pos[0], f_pos[1]), (n, n))
    ur, ui = transmitted(f_win, wave)
    wave_lr, wave_li = left_sums(ur, ui, tall)
    adj_lr, adj_li = left_sums(adjoint[0], adjoint[1], tall)
    for tick in range(TICKS):
        a_pos = lax.dynamic_slice(spots, (tick + section, 0), (1, 2))[0]
        a_win = lax.dynamic_slice(extent, (a_pos[0], a_pos[1]), (n, n))
        fwd_r, fwd_i = forward_middle(
            wave_lr, wave_li, intensity[0, tick], is_last, tall, broad, prop_r, prop_i, n
        )
        bwd_r, bwd_i = backward_middle(adj_lr, adj_li, tall, broad, prop_r, prop_i, n)
        more = tick + 1 < TICKS
        if more:
            n_pos = lax.dynamic_slice(spots, (tick + 1 - section + 2 * sections - 1, 0), (1, 2))[0]
            n_win = lax.dynamic_slice(extent, (n_pos[0], n_pos[1]), (n, n))
            wave_lr = jnp.zeros((2 * n, n), jnp.float32)
            wave_li = jnp.zeros((2 * n, n), jnp.float32)
            adj_lr = jnp.zeros((2 * n, n), jnp.float32)
            adj_li = jnp.zeros((2 * n, n), jnp.float32)
        sent_r, sent_i = right_rows(fwd_r, fwd_i, broad, -1.0, n)
        sent = jnp.stack([sent_r, sent_i])
        back, delta = backward_rows(
            bwd_r, bwd_i, saved_wave[0, 0, tick, :, 0:rows], a_win, broad, n
        )
        back_half = back.astype(jnp.bfloat16)
        moved = shifted(sent.astype(jnp.bfloat16), "depth", 1).astype(sent.dtype)
        returned = shifted(back_half, "depth", -1)
        wave_rows = jnp.where(is_first, probe_wave, moved)
        adj_rows = jnp.where(is_last, sent.astype(jnp.bfloat16), returned)
        if more:
            nr, ni = transmitted(n_win, wave_rows)
            part_r, part_i = left_sums(nr, ni, tall)
            wave_lr = part_r
            wave_li = part_i
            part_r, part_i = left_sums(adj_rows[0], adj_rows[1], tall)
            adj_lr = part_r
            adj_li = part_i
        delta_parts = delta
        wave = wave_rows
        adjoint = adj_rows
        delta = delta_parts
        total = place(total, delta, a_pos)
    core_sum = fold_final(total, core, margin)
    return (wave[None, None], adjoint[None, None], core_sum[None])


def solution(mesh):
    placed = (
        P("depth", "tile", None),
        P(),
        P("tile", None, None),
        P("tile", None, None, None),
        P("depth", "tile", None, None, None),
        P("depth", "tile", None, None, None),
        P("depth", "tile", None, None, None, None),
    )
    return jax.shard_map(
        on_device,
        mesh=mesh,
        in_specs=placed,
        out_specs=(
            P("depth", "tile", None, None, None),
            P("depth", "tile", None, None, None),
            P("depth", "tile", None),
        ),
        check_vma=False,
    )
```

profile of v0, /device:TPU:1, one launch (start us, length us, event | category | flops | bytes accessed | tf_op | source)
XLA Modules:
  0.0 140.5 jit_solution(3728302083068790434)
XLA Ops:
  1.7 1.3 collective-permute-start.1
  3.0 4.6 %collective-permute-start = (bf16[64,384]{1,0:T(8,128)(2,1)S(1)}, bf16[64,384]{1,0:T(8,128)(2,1)S(1)}, u32[]{:S(2)}, u32[]{:S(2)}) collective-permute-start(bf16[64,384]{1,0:T(8,128)(2,1)S(1)} %get-tuple-element.41), channel_id=1, source_target_pairs={{0,1},{1,2},{2,3},{4,5},{5,6},{6,7},{8,9},{9,10},{10,11},{12,13},{... | collective-permute-start | bytes 147464 | tf_op jit(solution)/shard_map/ppermute | solution.py:26
  9.7 1.3 fusion.144
  11.0 1.3 fusion.145
  50.3 2.2 %fusion.6 = (f32[256,256]{1,0:T(8,128)S(1)}, bf16[1,256,256]{2,1,0:T(8,128)(2,1)S(1)}, bf16[1,256,256]{2,1,0:T(8,128)(2,1)S(1)}) fusion(f32[384,384]{1,0:T(8,128)S(1)} %maximum_convert_fusion, s32[]{:T(128)S(6)} %select_n.288, s32[]{:T(128)S(6)} %select_n.289, bf16[1,1,4,2,256,256]{5,4,3,2,1,0:T(8,128)(2,1)} %param.13, f32[256,512]{1,0:T(8,128)S(1)} %fusion.202, ...), kind=kLoop, calls=%fused_computation.39 | loop fusion | flops 1638400 | bytes 2097160 | tf_op jit(solution)/shard_map/mul | solution.py:99
  52.5 3.0 %collective-permute-start.6 = (bf16[2,256,256]{2,1,0:T(8,128)(2,1)S(1)}, bf16[2,256,256]{2,1,0:T(8,128)(2,1)}, u32[]{:S(2)}, u32[]{:S(2)}) collective-permute-start(bf16[2,256,256]{2,1,0:T(8,128)(2,1)S(1)} %pad_maximum_fusion.6), channel_id=1, source_target_pairs={{4,0},{8,4},{12,8},{16,12},{20,16},{24,20},{28,24},{5,1},{9,5},{13... | collective-permute-start | bytes 786440 | tf_op jit(solution)/shard_map/ppermute | solution.py:18
  56.1 3.9 %dynamic_update_slice.12 = f32[384,384]{1,0:T(8,128)S(1)} dynamic-update-slice(f32[384,384]{1,0:T(8,128)S(1)} %broadcast_in_dim.20, f32[256,256]{1,0:T(8,128)S(1)} %get-tuple-element.12, s32[]{:T(128)S(6)} %select_n.288, s32[]{:T(128)S(6)} %select_n.289) | dynamic-update-slice | bytes 524292 | tf_op jit(solution)/shard_map/dynamic_update_slice | solution.py:113
  63.2 1.3 fusion.146
  64.4 1.3 fusion.147
  66.2 2.5 %collective-permute-start.2 = (bf16[2,256,256]{2,1,0:T(8,128)(2,1)S(1)}, bf16[2,256,256]{2,1,0:T(8,128)(2,1)S(1)}, u32[]{:S(2)}, u32[]{:S(2)}) collective-permute-start(bf16[2,256,256]{2,1,0:T(8,128)(2,1)S(1)} %get-tuple-element.40), channel_id=1, source_target_pairs={{0,4},{4,8},{8,12},{12,16},{16,20},{20,24},{24,28},{1,5},{5,9},{9,... | collective-permute-start | bytes 786440 | tf_op jit(solution)/shard_map/ppermute | solution.py:18
  68.7 2.2 %fusion.13 = (f32[256,256]{1,0:T(8,128)S(1)}, bf16[1,256,256]{2,1,0:T(8,128)(2,1)S(1)}, bf16[1,256,256]{2,1,0:T(8,128)(2,1)S(1)}) fusion(f32[384,384]{1,0:T(8,128)S(1)} %dynamic_update_slice.12, s32[]{:T(128)S(6)} %select_n.285, s32[]{:T(128)S(6)} %select_n.286, f32[384,384]{1,0:T(8,128)S(1)} %maximum_convert_fusion, ...), kind=kLoop, calls=%fused_computation.46 | loop fusion | flops 1703936 | bytes 2359304 | tf_op jit(solution)/shard_map/add | solution.py:113
  71.0 3.9 %dynamic_update_slice.13 = f32[384,384]{1,0:T(8,128)S(1)} dynamic-update-slice(f32[384,384]{1,0:T(8,128)S(1)} %dynamic_update_slice.12, f32[256,256]{1,0:T(8,128)S(1)} %get-tuple-element.9, s32[]{:T(128)S(6)} %select_n.285, s32[]{:T(128)S(6)} %select_n.286) | dynamic-update-slice | bytes 524292 | tf_op jit(solution)/shard_map/dynamic_update_slice | solution.py:113
  74.9 2.3 %collective-permute-start.7 = (bf16[2,256,256]{2,1,0:T(8,128)(2,1)S(1)}, bf16[2,256,256]{2,1,0:T(8,128)(2,1)S(1)}, u32[]{:S(2)}, u32[]{:S(2)}) collective-permute-start(bf16[2,256,256]{2,1,0:T(8,128)(2,1)S(1)} %pad_maximum_fusion.7), channel_id=1, source_target_pairs={{4,0},{8,4},{12,8},{16,12},{20,16},{24,20},{28,24},{5,1},{9,5},{13... | collective-permute-start | bytes 786440 | tf_op jit(solution)/shard_map/ppermute | solution.py:18
  83.7 1.3 fusion.148
  85.0 1.3 fusion.149
  86.7 3.5 %collective-permute-start.3 = (bf16[2,256,256]{2,1,0:T(8,128)(2,1)S(1)}, bf16[2,256,256]{2,1,0:T(8,128)(2,1)S(1)}, u32[]{:S(2)}, u32[]{:S(2)}) collective-permute-start(bf16[2,256,256]{2,1,0:T(8,128)(2,1)S(1)} %get-tuple-element.38), channel_id=1, source_target_pairs={{0,4},{4,8},{8,12},{12,16},{16,20},{20,24},{24,28},{1,5},{5,9},{9,... | collective-permute-start | bytes 786440 | tf_op jit(solution)/shard_map/ppermute | solution.py:18
  90.2 2.2 %fusion.20 = (f32[256,256]{1,0:T(8,128)S(1)}, bf16[1,256,256]{2,1,0:T(8,128)(2,1)S(1)}, bf16[1,256,256]{2,1,0:T(8,128)(2,1)S(1)}) fusion(f32[384,384]{1,0:T(8,128)S(1)} %dynamic_update_slice.13, s32[]{:T(128)S(6)} %select_n.282, s32[]{:T(128)S(6)} %select_n.283, f32[384,384]{1,0:T(8,128)S(1)} %maximum_convert_fusion, ...), kind=kLoop, calls=%fused_computation.53 | loop fusion | flops 1703936 | bytes 2359304 | tf_op jit(solution)/shard_map/add | solution.py:113
  92.5 3.9 %dynamic_update_slice.14 = f32[384,384]{1,0:T(8,128)S(1)} dynamic-update-slice(f32[384,384]{1,0:T(8,128)S(1)} %dynamic_update_slice.13, f32[256,256]{1,0:T(8,128)S(1)} %get-tuple-element.6, s32[]{:T(128)S(6)} %select_n.282, s32[]{:T(128)S(6)} %select_n.283) | dynamic-update-slice | bytes 524292 | tf_op jit(solution)/shard_map/dynamic_update_slice | solution.py:113
  96.4 2.2 %collective-permute-start.8 = (bf16[2,256,256]{2,1,0:T(8,128)(2,1)S(1)}, bf16[2,256,256]{2,1,0:T(8,128)(2,1)S(1)}, u32[]{:S(2)}, u32[]{:S(2)}) collective-permute-start(bf16[2,256,256]{2,1,0:T(8,128)(2,1)S(1)} %pad_maximum_fusion.8), channel_id=1, source_target_pairs={{4,0},{8,4},{12,8},{16,12},{20,16},{24,20},{28,24},{5,1},{9,5},{13... | collective-permute-start | bytes 786440 | tf_op jit(solution)/shard_map/ppermute | solution.py:18
  98.6 1.2 fusion.140
  99.9 1.2 fusion.141
  105.0 1.3 fusion.150
  106.3 1.3 fusion.151
  108.1 3.5 %collective-permute-start.4 = (bf16[2,256,256]{2,1,0:T(8,128)(2,1)S(1)}, bf16[2,256,256]{2,1,0:T(8,128)(2,1)}, u32[]{:S(2)}, u32[]{:S(2)}) collective-permute-start(bf16[2,256,256]{2,1,0:T(8,128)(2,1)S(1)} %get-tuple-element.36), channel_id=1, source_target_pairs={{0,4},{4,8},{8,12},{12,16},{16,20},{20,24},{24,28},{1,5},{5,9},{9,... | collective-permute-start | bytes 786440 | tf_op jit(solution)/shard_map/ppermute | solution.py:18
  111.6 2.2 %fusion.27 = (f32[256,256]{1,0:T(8,128)S(1)}, bf16[1,256,256]{2,1,0:T(8,128)(2,1)S(1)}, bf16[1,256,256]{2,1,0:T(8,128)(2,1)S(1)}) fusion(f32[384,384]{1,0:T(8,128)S(1)} %dynamic_update_slice.14, s32[]{:T(128)S(6)} %select_n.279, s32[]{:T(128)S(6)} %select_n.280, f32[384,384]{1,0:T(8,128)S(1)} %maximum_convert_fusion, ...), kind=kLoop, calls=%fused_computation.60 | loop fusion | flops 1703936 | bytes 2359304 | tf_op jit(solution)/shard_map/add | solution.py:113
  113.9 1.9 %collective-permute-start.9 = (bf16[2,256,256]{2,1,0:T(8,128)(2,1)S(1)}, bf16[2,256,256]{2,1,0:T(8,128)(2,1)S(1)}, u32[]{:S(2)}, u32[]{:S(2)}) collective-permute-start(bf16[2,256,256]{2,1,0:T(8,128)(2,1)S(1)} %pad_maximum_fusion.9), channel_id=1, source_target_pairs={{4,0},{8,4},{12,8},{16,12},{20,16},{24,20},{28,24},{5,1},{9,5},{13... | collective-permute-start | bytes 786440 | tf_op jit(solution)/shard_map/ppermute | solution.py:18
  115.8 3.6 %dynamic_update_slice.15 = f32[384,384]{1,0:T(8,128)S(1)} dynamic-update-slice(f32[384,384]{1,0:T(8,128)S(1)} %dynamic_update_slice.14, f32[256,256]{1,0:T(8,128)S(1)} %get-tuple-element.3, s32[]{:T(128)S(6)} %select_n.279, s32[]{:T(128)S(6)} %select_n.280) | dynamic-update-slice | bytes 524292 | tf_op jit(solution)/shard_map/dynamic_update_slice | solution.py:113
  119.5 1.3 collective-permute-start.11
  120.8 4.4 %collective-permute-start.10 = (bf16[64,384]{1,0:T(8,128)(2,1)S(1)}, bf16[64,384]{1,0:T(8,128)(2,1)S(1)}, u32[]{:S(2)}, u32[]{:S(2)}) collective-permute-start(bf16[64,384]{1,0:T(8,128)(2,1)S(1)} %get-tuple-element.31), channel_id=1, source_target_pairs={{0,1},{1,2},{2,3},{4,5},{5,6},{6,7},{8,9},{9,10},{10,11},{12,13},{... | collective-permute-start | bytes 147464 | tf_op jit(solution)/shard_map/ppermute | solution.py:18
  127.4 1.2 fusion.143
  132.2 4.2 %collective-permute-start.5 = (bf16[2,256,256]{2,1,0:T(8,128)(2,1)S(1)}, bf16[2,256,256]{2,1,0:T(8,128)(2,1)S(1)}, u32[]{:S(2)}, u32[]{:S(2)}) collective-permute-start(bf16[2,256,256]{2,1,0:T(8,128)(2,1)S(1)} %get-tuple-element.34), channel_id=1, source_target_pairs={{0,4},{4,8},{8,12},{12,16},{16,20},{20,24},{24,28},{1,5},{5,9},{9,... | collective-permute-start | bytes 786440 | tf_op jit(solution)/shard_map/ppermute | solution.py:18
  137.2 2.5 %collective-permute-done.5 = bf16[2,256,256]{2,1,0:T(8,128)(2,1)S(1)} collective-permute-done((bf16[2,256,256]{2,1,0:T(8,128)(2,1)S(1)}, bf16[2,256,256]{2,1,0:T(8,128)(2,1)S(1)}, u32[]{:S(2)}, u32[]{:S(2)}) %collective-permute-start.5) | collective-permute-done | bytes 262176 | tf_op jit(solution)/shard_map/ppermute | solution.py:18
  (111 shorter events, 34.1 us)
Async XLA Ops:
  0.6 7.0 %copy-start.2 = (f32[1,256,384]{2,1,0:T(8,128)S(1)}, f32[1,256,384]{2,1,0:T(8,128)}, u32[]{:S(2)}) copy-start(f32[1,256,384]{2,1,0:T(8,128)} %param.7) | copy-start | bytes 1179652
  1.7 43.7 %collective-permute-start.1 = (bf16[64,384]{1,0:T(8,128)(2,1)S(1)}, bf16[64,384]{1,0:T(8,128)(2,1)S(1)}, u32[]{:S(2)}, u32[]{:S(2)}) collective-permute-start(bf16[64,384]{1,0:T(8,128)(2,1)S(1)} %get-tuple-element.42), channel_id=1, source_target_pairs={{1,0},{2,1},{3,2},{5,4},{6,5},{7,6},{9,8},{10,9},{11,10},{13,12},{... | collective-permute-start | bytes 147464 | tf_op jit(solution)/shard_map/ppermute | solution.py:29
  3.0 42.4 %collective-permute-start = (bf16[64,384]{1,0:T(8,128)(2,1)S(1)}, bf16[64,384]{1,0:T(8,128)(2,1)S(1)}, u32[]{:S(2)}, u32[]{:S(2)}) collective-permute-start(bf16[64,384]{1,0:T(8,128)(2,1)S(1)} %get-tuple-element.41), channel_id=1, source_target_pairs={{0,1},{1,2},{2,3},{4,5},{5,6},{6,7},{8,9},{9,10},{10,11},{12,13},{... | collective-permute-start | bytes 147464 | tf_op jit(solution)/shard_map/ppermute | solution.py:26
  7.7 1.1 copy-start.4
  12.8 0.7 copy-start.5
  15.3 30.3 %copy-start.3 = (f32[1,1,2,256,256]{4,3,2,1,0:T(8,128)S(1)}, f32[1,1,2,256,256]{4,3,2,1,0:T(8,128)}, u32[]{:S(2)}) copy-start(f32[1,1,2,256,256]{4,3,2,1,0:T(8,128)} %param.11) | copy-start | bytes 1572868
  48.5 1.2 copy-start.1
  52.5 8.7 %collective-permute-start.6 = (bf16[2,256,256]{2,1,0:T(8,128)(2,1)S(1)}, bf16[2,256,256]{2,1,0:T(8,128)(2,1)}, u32[]{:S(2)}, u32[]{:S(2)}) collective-permute-start(bf16[2,256,256]{2,1,0:T(8,128)(2,1)S(1)} %pad_maximum_fusion.6), channel_id=1, source_target_pairs={{4,0},{8,4},{12,8},{16,12},{20,16},{24,20},{28,24},{5,1},{9,5},{13... | collective-permute-start | bytes 786440 | tf_op jit(solution)/shard_map/ppermute | solution.py:18
  66.2 11.0 %collective-permute-start.2 = (bf16[2,256,256]{2,1,0:T(8,128)(2,1)S(1)}, bf16[2,256,256]{2,1,0:T(8,128)(2,1)S(1)}, u32[]{:S(2)}, u32[]{:S(2)}) collective-permute-start(bf16[2,256,256]{2,1,0:T(8,128)(2,1)S(1)} %get-tuple-element.40), channel_id=1, source_target_pairs={{0,4},{4,8},{8,12},{12,16},{16,20},{20,24},{24,28},{1,5},{5,9},{9,... | collective-permute-start | bytes 786440 | tf_op jit(solution)/shard_map/ppermute | solution.py:18
  74.9 2.3 %copy-start = (bf16[2,256,256]{2,1,0:T(8,128)(2,1)S(1)}, bf16[2,256,256]{2,1,0:T(8,128)(2,1)}, u32[]{:S(2)}) copy-start(bf16[2,256,256]{2,1,0:T(8,128)(2,1)} %param.8) | copy-start | bytes 786436
  74.9 7.8 %collective-permute-start.7 = (bf16[2,256,256]{2,1,0:T(8,128)(2,1)S(1)}, bf16[2,256,256]{2,1,0:T(8,128)(2,1)S(1)}, u32[]{:S(2)}, u32[]{:S(2)}) collective-permute-start(bf16[2,256,256]{2,1,0:T(8,128)(2,1)S(1)} %pad_maximum_fusion.7), channel_id=1, source_target_pairs={{4,0},{8,4},{12,8},{16,12},{20,16},{24,20},{28,24},{5,1},{9,5},{13... | collective-permute-start | bytes 786440 | tf_op jit(solution)/shard_map/ppermute | solution.py:18
  86.7 11.8 %collective-permute-start.3 = (bf16[2,256,256]{2,1,0:T(8,128)(2,1)S(1)}, bf16[2,256,256]{2,1,0:T(8,128)(2,1)S(1)}, u32[]{:S(2)}, u32[]{:S(2)}) collective-permute-start(bf16[2,256,256]{2,1,0:T(8,128)(2,1)S(1)} %get-tuple-element.38), channel_id=1, source_target_pairs={{0,4},{4,8},{8,12},{12,16},{16,20},{20,24},{24,28},{1,5},{5,9},{9,... | collective-permute-start | bytes 786440 | tf_op jit(solution)/shard_map/ppermute | solution.py:18
  96.4 7.7 %collective-permute-start.8 = (bf16[2,256,256]{2,1,0:T(8,128)(2,1)S(1)}, bf16[2,256,256]{2,1,0:T(8,128)(2,1)S(1)}, u32[]{:S(2)}, u32[]{:S(2)}) collective-permute-start(bf16[2,256,256]{2,1,0:T(8,128)(2,1)S(1)} %pad_maximum_fusion.8), channel_id=1, source_target_pairs={{4,0},{8,4},{12,8},{16,12},{20,16},{24,20},{28,24},{5,1},{9,5},{13... | collective-permute-start | bytes 786440 | tf_op jit(solution)/shard_map/ppermute | solution.py:18
  108.1 17.1 %collective-permute-start.4 = (bf16[2,256,256]{2,1,0:T(8,128)(2,1)S(1)}, bf16[2,256,256]{2,1,0:T(8,128)(2,1)}, u32[]{:S(2)}, u32[]{:S(2)}) collective-permute-start(bf16[2,256,256]{2,1,0:T(8,128)(2,1)S(1)} %get-tuple-element.36), channel_id=1, source_target_pairs={{0,4},{4,8},{8,12},{12,16},{16,20},{20,24},{24,28},{1,5},{5,9},{9,... | collective-permute-start | bytes 786440 | tf_op jit(solution)/shard_map/ppermute | solution.py:18
  113.9 17.6 %collective-permute-start.9 = (bf16[2,256,256]{2,1,0:T(8,128)(2,1)S(1)}, bf16[2,256,256]{2,1,0:T(8,128)(2,1)S(1)}, u32[]{:S(2)}, u32[]{:S(2)}) collective-permute-start(bf16[2,256,256]{2,1,0:T(8,128)(2,1)S(1)} %pad_maximum_fusion.9), channel_id=1, source_target_pairs={{4,0},{8,4},{12,8},{16,12},{20,16},{24,20},{28,24},{5,1},{9,5},{13... | collective-permute-start | bytes 786440 | tf_op jit(solution)/shard_map/ppermute | solution.py:18
  119.5 16.9 %collective-permute-start.11 = (bf16[64,384]{1,0:T(8,128)(2,1)S(1)}, bf16[64,384]{1,0:T(8,128)(2,1)S(1)}, u32[]{:S(2)}, u32[]{:S(2)}) collective-permute-start(bf16[64,384]{1,0:T(8,128)(2,1)S(1)} %get-tuple-element.32), channel_id=1, source_target_pairs={{1,0},{2,1},{3,2},{5,4},{6,5},{7,6},{9,8},{10,9},{11,10},{13,12},{... | collective-permute-start | bytes 147464 | tf_op jit(solution)/shard_map/ppermute | solution.py:18
  120.8 15.6 %collective-permute-start.10 = (bf16[64,384]{1,0:T(8,128)(2,1)S(1)}, bf16[64,384]{1,0:T(8,128)(2,1)S(1)}, u32[]{:S(2)}, u32[]{:S(2)}) collective-permute-start(bf16[64,384]{1,0:T(8,128)(2,1)S(1)} %get-tuple-element.31), channel_id=1, source_target_pairs={{0,1},{1,2},{2,3},{4,5},{5,6},{6,7},{8,9},{9,10},{10,11},{12,13},{... | collective-permute-start | bytes 147464 | tf_op jit(solution)/shard_map/ppermute | solution.py:18
  132.2 7.5 %collective-permute-start.5 = (bf16[2,256,256]{2,1,0:T(8,128)(2,1)S(1)}, bf16[2,256,256]{2,1,0:T(8,128)(2,1)S(1)}, u32[]{:S(2)}, u32[]{:S(2)}) collective-permute-start(bf16[2,256,256]{2,1,0:T(8,128)(2,1)S(1)} %get-tuple-element.34), channel_id=1, source_target_pairs={{0,4},{4,8},{8,12},{12,16},{16,20},{20,24},{24,28},{1,5},{5,9},{9,... | collective-permute-start | bytes 786440 | tf_op jit(solution)/shard_map/ppermute | solution.py:18
where the time goes:
time: 143 us; the launch traced here: 141 us
  starting transfers between devices  34.5 us (24%)
  matrix products  31.3 us (22%)
  between operations  31.2 us (22%)
  other arithmetic  21 us (15%)
  local copies, waits for them, and re-layouts  18.4 us (13%)
  waiting for transfers between devices  4.1 us (3%)
    ppermute x10, starting transfers between devices, shifted(): return lax.ppermute(block, axis, route)  28.7 us
    dynamic_update_slice x4, local copies, waits for them, and re-layouts, place(): return lax.dynamic_update_slice(grad, old + delta, (corner[0], corner[1]))  15.2 us
    dot_general x16, matrix products, left_sums(): jnp.dot(tall_cols, imag.astype(jnp.bfloat16), preferred_element_type=jnp....  12 us
    dot_general x16, matrix products, left_sums(): jnp.dot(tall_cols, real.astype(jnp.bfloat16), preferred_element_type=jnp....  12 us
    add x3, other arithmetic, place(): return lax.dynamic_update_slice(grad, old + delta, (corner[0], corner[1]))  6.73 us
    sub x4, other arithmetic, forward_middle(): far_r = big_r * prop_r - big_i * prop_i  4.76 us
    ppermute x1, starting transfers between devices, with_halo(): lax.ppermute(lax.slice_in_dim(block, block.shape[dim] - width, None, axis...  4.56 us
    ppermute x10, waiting for transfers between devices, shifted(): return lax.ppermute(block, axis, route)  4.09 us
  transfers between devices with their start and end apart: 12, of which 4 were waited for; matrix products, arithmetic and copies ran while one was open for 34% of the time, Pallas kernels for 0%

commit v1 on v0

v1 whole, which is shorter than its diff:
```python
import functools
import math

import jax
import jax.numpy as jnp
import numpy as np
from jax import lax
from jax.experimental import pallas as pl
from jax.experimental.pallas import tpu as pltpu
from jax.sharding import PartitionSpec as P

SIGMA = 0.8
DEFOCUS = 6.0
ROWS = 128
STEP = 32
MESH = pl.DeviceIdType.MESH
F32 = jnp.float32
BF16 = jnp.bfloat16


def tables(n):
    idx = np.arange(n)
    angle = (idx[:, None] * idx[None, :] % n) * (2.0 * math.pi / n)
    scale = 1.0 / math.sqrt(n)
    cos_t = np.asarray((np.cos(angle) * scale).astype(BF16)).astype(np.float64)
    sin_t = np.asarray((np.sin(angle) * scale).astype(BF16)).astype(np.float64)
    freq = np.where(idx < n // 2, idx, idx - n).astype(np.float64)
    q = np.exp(-1j * math.pi * DEFOCUS * freq * freq / (n * n))
    f = cos_t - 1j * sin_t
    m = (np.conj(f) * q[None, :]) @ f
    m = (m + m.T) / 2
    g = np.conj(f) * q[None, :]
    parts = (m.real, m.imag, cos_t, -sin_t, g.real, g.imag, g.T.real, g.T.imag)
    return np.stack([p.astype(BF16) for p in parts])


def sin_cos(x):
    k = jnp.floor(x * (2.0 / math.pi) + 0.5)
    r = x - k * 1.5703125
    r = r - k * 4.837512969970703125e-4
    r = r - k * 7.54978995489188216e-8
    z = r * r
    s = r + r * z * (-1.6666654611e-1 + z * (8.3321608736e-3 + z * -1.9515295891e-4))
    c = 1.0 - 0.5 * z + z * z * (
        4.166664568298827e-2 + z * (-1.388731625493765e-3 + z * 2.443315711809948e-5)
    )
    half = jnp.floor(k * 0.5)
    odd = k - 2.0 * half > 0.5
    quarter = half - 2.0 * jnp.floor(half * 0.5)
    sign = 1.0 - 2.0 * quarter
    sin_v = jnp.where(odd, c, s) * sign
    cos_v = jnp.where(odd, -s, c) * sign
    return sin_v, cos_v


def dot(a, b):
    return jnp.dot(a, b, preferred_element_type=F32)


def kernel(
    sections, tiles,
    pos, pot, probe, inten, fwd, adj, saved, tab,
    o_fwd, o_adj, o_grad,
    in_f, in_b, out_f, out_b, l_f, r_f, l_b, r_b, l_g, r_g,
    ext, tf, ta, bk, total, a_buf, y_buf,
    halo_out, halo_in, edge_out, edge_in,
    send_f, recv_f, send_b, recv_b, send_h, recv_h, send_e, recv_e,
):
    n = probe.shape[1]
    nc = n // ROWS
    core, width = pot.shape[1], pot.shape[2]
    margin = (width - core) // 2
    ticks = inten.shape[1]
    s = lax.axis_index("depth")
    t = lax.axis_index("tile")
    first, last = s == 0, s == sections - 1
    low, high = t == 0, t == tiles - 1

    barrier = pltpu.get_barrier_semaphore()
    one = lambda c: jnp.where(c, 1, 0).astype(jnp.int32)

    def greet(cond, axis, to):
        @pl.when(cond)
        def _():
            pl.semaphore_signal(barrier, inc=1, device_id={axis: to}, device_id_type=MESH)

    greet(s > 0, "depth", s - 1)
    greet(s < sections - 1, "depth", s + 1)
    greet(t > 0, "tile", t - 1)
    greet(t < tiles - 1, "tile", t + 1)
    halo_out[0] = pot[0, 0:margin, :].astype(BF16)
    halo_out[1] = pot[0, core - margin : core, :].astype(BF16)
    pl.semaphore_wait(barrier, one(s > 0) + one(s < sections - 1) + one(t > 0) + one(t < tiles - 1))

    def hop(src, dst, ssem, rsem, axis, to):
        return pltpu.make_async_remote_copy(
            src_ref=src, dst_ref=dst, send_sem=ssem, recv_sem=rsem,
            device_id={axis: to}, device_id_type=MESH,
        )

    def tile_pair(src, dst, ssem, rsem):
        down = hop(src.at[0], dst.at[1], ssem.at[0], rsem.at[1], "tile", t - 1)
        up = hop(src.at[1], dst.at[0], ssem.at[1], rsem.at[0], "tile", t + 1)
        return down, up

    def tile_start(src, dst, ssem, rsem):
        down, up = tile_pair(src, dst, ssem, rsem)
        pl.when(t > 0)(down.start)
        pl.when(t < tiles - 1)(up.start)

    def tile_wait(src, dst, ssem, rsem):
        down, up = tile_pair(src, dst, ssem, rsem)

        @pl.when(t > 0)
        def _():
            down.wait_send()
            up.wait_recv()

        @pl.when(t < tiles - 1)
        def _():
            up.wait_send()
            down.wait_recv()

    tile_start(halo_out, halo_in, send_h, recv_h)

    def fill(l_ref, r_ref, lr, li, rr, ri):
        for c in range(nc):
            cols = slice(c * ROWS, (c + 1) * ROWS)
            l_ref[c, 0:n, 0:ROWS] = lr[:, cols]
            l_ref[c, 0:n, ROWS : 2 * ROWS] = -li[:, cols]
            l_ref[c, n : 2 * n, 0:ROWS] = li[:, cols]
            l_ref[c, n : 2 * n, ROWS : 2 * ROWS] = lr[:, cols]
        r_ref[0:n, 0:n] = rr
        r_ref[0:n, n : 2 * n] = ri
        r_ref[n : 2 * n, 0:n] = -ri
        r_ref[n : 2 * n, n : 2 * n] = rr

    fill(l_b, r_b, tab[0], -tab[1], tab[0], -tab[1])

    @pl.when(jnp.logical_not(last))
    def _():
        fill(l_f, r_f, tab[0], tab[1], tab[0], tab[1])

    @pl.when(last)
    def _():
        fill(l_f, r_f, tab[2], tab[3], tab[2], tab[3])
        fill(l_g, r_g, tab[4], tab[5], tab[6], tab[7])

    for c in range(nc):
        for part in range(2):
            rows = slice(c * ROWS, (c + 1) * ROWS)
            to = slice(part * ROWS, (part + 1) * ROWS)
            in_f[0, c, to, :] = fwd[0, 0, part, rows, :].astype(BF16)
            in_b[0, c, to, :] = adj[0, 0, part, rows, :]

    @pl.when(first)
    def _():
        for k in range(ticks):
            for c in range(nc):
                in_f[k + 1, c] = jnp.concatenate(
                    [probe[part, c * ROWS : (c + 1) * ROWS, :] for part in range(2)], axis=0
                )

    total[...] = jnp.zeros_like(total)
    ext[margin : margin + core, :] = pot[0].astype(BF16)

    @pl.when(low)
    def _():
        halo_in[0] = jnp.zeros((margin, width), BF16)
        edge_in[0] = jnp.zeros((margin, width), BF16)

    @pl.when(high)
    def _():
        halo_in[1] = jnp.zeros((margin, width), BF16)
        edge_in[1] = jnp.zeros((margin, width), BF16)

    tile_wait(halo_out, halo_in, send_h, recv_h)
    ext[0:margin, :] = halo_in[0]
    ext[margin + core :, :] = halo_in[1]

    def chosen(offset, axis):
        shape = (n, width) if axis else (width, n)
        ahead = lax.broadcasted_iota(jnp.int32, shape, axis) - lax.broadcasted_iota(
            jnp.int32, shape, 1 - axis
        )
        return jnp.where(ahead == offset, 1.0, 0.0).astype(BF16)

    def window(index, out):
        rows = dot(chosen(pos[0, index, 0], 1), ext[...]).astype(BF16)
        bk[0] = SIGMA * dot(rows, chosen(pos[0, index, 1], 0))
        for at in range(0, n, STEP):
            sv, cv = sin_cos(bk[0, at : at + STEP, :])
            out[0, at : at + STEP, :] = cv
            out[1, at : at + STEP, :] = sv

    def copy_f(k, c):
        return hop(out_f.at[k, c], in_f.at[k + 1, c], send_f.at[k, c], recv_f.at[k, c], "depth", s + 1)

    def copy_b(k, c):
        return hop(out_b.at[k, c], in_b.at[k + 1, c], send_b.at[k, c], recv_b.at[k, c], "depth", s - 1)

    def right(r_ref, c):
        rows = slice(c * ROWS, (c + 1) * ROWS)
        more = slice(n + c * ROWS, n + (c + 1) * ROWS)
        return dot(jnp.concatenate([a_buf[rows, :], a_buf[more, :]], axis=1), r_ref[...])

    def tick(k, carry):
        window(k + s, ta)
        window(k - s + 2 * sections - 1, tf)
        acc = None
        for c in range(nc):
            @pl.when(jnp.logical_and(k > 0, jnp.logical_not(last)))
            def _():
                copy_b(k - 1, c).wait_recv()
            term = dot(l_b[c], in_b[k, c])
            acc = term if acc is None else acc + term
        a_buf[...] = acc.astype(BF16)
        for c in range(nc):
            rows = slice(c * ROWS, (c + 1) * ROWS)
            lu = right(r_b, c)
            lur, lui = lu[:, 0:n], lu[:, n : 2 * n]
            tr, ti = ta[0, rows, :], ta[1, rows, :]
            br = tr * lur + ti * lui
            bi = tr * lui - ti * lur
            bk[0, rows, :] = br
            bk[1, rows, :] = bi
            out_b[k, c, 0:ROWS, :] = br.astype(BF16)
            out_b[k, c, ROWS : 2 * ROWS, :] = bi.astype(BF16)

            @pl.when(jnp.logical_not(first))
            def _():
                copy_b(k, c).start()
        acc = None
        for c in range(nc):
            rows = slice(c * ROWS, (c + 1) * ROWS)

            @pl.when(jnp.logical_and(k > 0, jnp.logical_not(first)))
            def _():
                copy_f(k - 1, c).wait_recv()
            wr = in_f[k, c, 0:ROWS, :].astype(F32)
            wi = in_f[k, c, ROWS : 2 * ROWS, :].astype(F32)
            tr, ti = tf[0, rows, :], tf[1, rows, :]
            u = jnp.concatenate([tr * wr - ti * wi, tr * wi + ti * wr], axis=0).astype(BF16)
            term = dot(l_f[c], u)
            acc = term if acc is None else acc + term
        a_buf[...] = acc.astype(BF16)

        @pl.when(jnp.logical_not(last))
        def _():
            for c in range(nc):
                out = right(r_f, c)
                out_f[k, c, 0:ROWS, :] = out[:, 0:n].astype(BF16)
                out_f[k, c, ROWS : 2 * ROWS, :] = out[:, n : 2 * n].astype(BF16)
                copy_f(k, c).start()

        @pl.when(last)
        def _():
            for c in range(nc):
                rows = slice(c * ROWS, (c + 1) * ROWS)
                out = right(r_f, c)
                vr, vi = out[:, 0:n], out[:, n : 2 * n]
                excess = vr * vr + vi * vi - inten[0, k, rows, :].astype(F32)
                y_buf[c, 0:ROWS, :] = (excess * vr).astype(BF16)
                y_buf[c, ROWS : 2 * ROWS, :] = (excess * vi).astype(BF16)
            left = None
            for c in range(nc):
                term = dot(l_g[c], y_buf[c])
                left = term if left is None else left + term
            a_buf[...] = left.astype(BF16)
            for c in range(nc):
                out = right(r_g, c)
                in_b[k + 1, c, 0:ROWS, :] = out[:, 0:n].astype(BF16)
                in_b[k + 1, c, ROWS : 2 * ROWS, :] = out[:, n : 2 * n].astype(BF16)

        sr = saved[0, 0, k, 0].astype(F32)
        si = saved[0, 0, k, 1].astype(F32)
        delta = SIGMA * (bk[1] * sr - bk[0] * si)
        coarse = delta.astype(BF16)
        fine = (delta - coarse.astype(F32)).astype(BF16)
        tall = dot(chosen(pos[0, k + s, 0], 0), jnp.concatenate([coarse, fine], axis=1)).astype(BF16)
        across = chosen(pos[0, k + s, 1], 1)
        total[...] += dot(tall[:, 0:n], across) + dot(tall[:, n : 2 * n], across)
        return carry

    lax.fori_loop(0, ticks, tick, 0)

    edge_out[0] = total[0:margin, :].astype(BF16)
    edge_out[1] = total[margin + core :, :].astype(BF16)
    tile_start(edge_out, edge_in, send_e, recv_e)
    o_grad[0, margin : core - margin, :] = total[2 * margin : core, :]
    tile_wait(edge_out, edge_in, send_e, recv_e)
    o_grad[0, 0:margin, :] = total[margin : 2 * margin, :] + edge_in[0].astype(F32)
    o_grad[0, core - margin : core, :] = total[core : core + margin, :] + edge_in[1].astype(F32)
    for c in range(nc):
        rows = slice(c * ROWS, (c + 1) * ROWS)

        @pl.when(jnp.logical_not(last))
        def _():
            copy_b(ticks - 1, c).wait_recv()
        o_adj[0, 0, 0, rows, :] = in_b[ticks, c, 0:ROWS, :]
        o_adj[0, 0, 1, rows, :] = in_b[ticks, c, ROWS : 2 * ROWS, :]

        @pl.when(jnp.logical_not(first))
        def _():
            copy_f(ticks - 1, c).wait_recv()
        o_fwd[0, 0, 0, rows, :] = in_f[ticks, c, 0:ROWS, :].astype(F32)
        o_fwd[0, 0, 1, rows, :] = in_f[ticks, c, ROWS : 2 * ROWS, :].astype(F32)
    for k in range(ticks):
        for c in range(nc):
            @pl.when(jnp.logical_not(last))
            def _():
                copy_f(k, c).wait_send()

            @pl.when(jnp.logical_not(first))
            def _():
                copy_b(k, c).wait_send()


def on_device(sections, tiles, potential, probe, positions, intensity, fwd_wave, adj_wave, saved_wave):
    n = probe.shape[1]
    nc = n // ROWS
    ticks = intensity.shape[1]
    core, width = potential.shape[1], potential.shape[2]
    margin = (width - core) // 2
    vmem = pl.BlockSpec(memory_space=pltpu.VMEM)
    smem = pl.BlockSpec(memory_space=pltpu.SMEM)
    dma = lambda *shape: pltpu.SemaphoreType.DMA(shape)
    wave = lambda count: pltpu.VMEM((count, nc, 2 * ROWS, n), BF16)
    lt = pltpu.VMEM((nc, 2 * n, 2 * ROWS), BF16)
    rt = pltpu.VMEM((2 * n, 2 * n), BF16)
    two = pltpu.VMEM((2, n, n), F32)
    strip = pltpu.VMEM((2, margin, width), BF16)
    return pl.pallas_call(
        functools.partial(kernel, sections, tiles),
        out_shape=(
            jax.ShapeDtypeStruct(fwd_wave.shape, F32),
            jax.ShapeDtypeStruct(adj_wave.shape, BF16),
            jax.ShapeDtypeStruct(potential.shape, F32),
        ),
        in_specs=[smem] + [vmem] * 7,
        out_specs=(vmem, vmem, vmem),
        scratch_shapes=[
            wave(ticks + 1), wave(ticks + 1), wave(ticks), wave(ticks),
            lt, rt, lt, rt, lt, rt,
            pltpu.VMEM((width, width), BF16), two, two, two,
            pltpu.VMEM((width, width), F32),
            pltpu.VMEM((2 * n, n), BF16),
            pltpu.VMEM((nc, 2 * ROWS, n), BF16),
            strip, strip, strip, strip,
            dma(ticks, nc), dma(ticks, nc), dma(ticks, nc), dma(ticks, nc),
            dma(2), dma(2), dma(2), dma(2),
        ],
        compiler_params=pltpu.CompilerParams(
            collective_id=0, has_side_effects=True, vmem_limit_bytes=60 * 1024 * 1024
        ),
        name="window",
    )(positions, potential, probe, intensity, fwd_wave, adj_wave, saved_wave, jnp.asarray(tables(n)))


def solution(mesh):
    placed = (
        P("depth", "tile", None),
        P(),
        P("tile", None, None),
        P("tile", None, None, None),
        P("depth", "tile", None, None, None),
        P("depth", "tile", None, None, None),
        P("depth", "tile", None, None, None, None),
    )
    return jax.shard_map(
        functools.partial(on_device, mesh.shape["depth"], mesh.shape["tile"]),
        mesh=mesh,
        in_specs=placed,
        out_specs=(
            P("depth", "tile", None, None, None),
            P("depth", "tile", None, None, None),
            P("depth", "tile", None),
        ),
        check_vma=False,
    )
```

time: 143 us -> 38 us (0.27); the launches traced: 141 us -> 37.8 us
  starting transfers between devices: 34.5 us -> 0 us
  Pallas kernels: 0 us -> 32 us
  matrix products: 31.3 us -> 0 us
  between operations: 31.2 us -> 0.65 us
  other arithmetic: 21 us -> 0 us
  local copies, waits for them, and re-layouts: 18.4 us -> 5.11 us
  waiting for transfers between devices: 4.1 us -> 0 us
    ppermute x12 -> x0, starting transfers between devices: 34.5 us -> none  [the longest x10 28.7 us: shifted(): return lax.ppermute(block, axis, route)]
    pallas_call x0 -> x1, Pallas kernels: none -> 32 us  [on_device(): pl.pallas_call(functools.partial(kernel, sections, tiles), out_shape=(jax...]
    dot_general x64 -> x0, matrix products: 31.3 us -> none  [the longest x16 12 us: left_sums(): jnp.dot(tall_cols, imag.astype(jnp.bfloat16), preferred_element_type=jnp....]
    dynamic_update_slice x4 -> x0, local copies, waits for them, and re-layouts: 15.2 us -> none  [place(): return lax.dynamic_update_slice(grad, old + delta, (corner[0], corner[1]))]
    add x3 -> x0, other arithmetic: 6.73 us -> none  [place(): return lax.dynamic_update_slice(grad, old + delta, (corner[0], corner[1]))]
    sub x4 -> x0, other arithmetic: 4.76 us -> none  [forward_middle(): far_r = big_r * prop_r - big_i * prop_i]
    unnamed x12 -> x8, local copies, waits for them, and re-layouts: 0.7 us -> 5.11 us
    ppermute x12 -> x0, waiting for transfers between devices: 4.1 us -> none  [the longest x10 4.09 us: shifted(): return lax.ppermute(block, axis, route)]
  transfers between devices with their start and end apart: 12 -> 0, of which waited for: 4 -> 0; matrix products, arithmetic and copies ran while one was open for 34% -> 0% of each run, Pallas kernels for 0% -> 0%
where the time goes in v1:
time: 38 us; the launch traced here: 37.8 us
  Pallas kernels  32 us (84%)
  local copies, waits for them, and re-layouts  5.11 us (13%)
  between operations  0.65 us (2%)
    pallas_call x1, Pallas kernels, on_device(): pl.pallas_call(functools.partial(kernel, sections, tiles), out_shape=(jax...  32 us
    unnamed x8, local copies, waits for them, and re-layouts  5.11 us

profile of v1, /device:TPU:1, one launch (start us, length us, event | category | flops | bytes accessed | tf_op | source)
XLA Modules:
  0.0 37.8 jit_solution(5289723218649337051)
XLA Ops:
  0.6 1.4 %copy.11.pos = s32[1,19,2]{2,1,0:T(8,128)} copy(s32[1,19,2]{1,2,0:T(2,128)} %param.10) | data formatting | bytes 304 | tf_op args[2]
  2.0 32.0 %window.1 = (f32[1,1,2,256,256]{4,3,2,1,0:T(8,128)}, bf16[1,1,2,256,256]{4,3,2,1,0:T(8,128)(2,1)}, f32[1,256,384]{2,1,0:T(8,128)}) custom-call(s32[1,19,2]{2,1,0:T(8,128)} %copy.11.pos, f32[1,256,384]{2,1,0:T(8,128)} %pot.1, bf16[2,256,256]{2,1,0:T(8,128)(2,1)} %probe.1, bf16[1,4,256,256]{3,2,1,0:T(8,128)(2,1)} %inten.1, f32[1,1,2,256,256]{4,3,2,1,0:T(8,128)} %fwd.1, ...), custom_call_target="tpu_custom_call" | custom-call | tf_op jit(solution)/shard_map/window/pallas_call | solution.py:333
  34.0 0.0 copy-start.1
  34.0 1.9 %copy.15 = f32[1,1,2,256,256]{4,3,2,1,0:T(8,128)} copy(f32[1,1,2,256,256]{4,3,2,1,0:T(8,128)} %get-tuple-element.6) | data formatting | bytes 1048576
  36.0 0.0 copy-done.1
  36.0 0.0 copy-start
  36.0 0.7 %copy.16 = bf16[1,1,2,256,256]{4,3,2,1,0:T(8,128)(2,1)} copy(bf16[1,1,2,256,256]{4,3,2,1,0:T(8,128)(2,1)S(1)} %copy-done.1) | data formatting | bytes 524288
  36.7 0.4 %copy-done = f32[1,256,384]{2,1,0:T(8,128)S(1)} copy-done((f32[1,256,384]{2,1,0:T(8,128)S(1)}, f32[1,256,384]{2,1,0:T(8,128)}, u32[]{:S(2)}) %copy-start) | copy-done | bytes 393240
  37.1 0.7 %copy.17 = f32[1,256,384]{2,1,0:T(8,128)} copy(f32[1,256,384]{2,1,0:T(8,128)S(1)} %copy-done) | data formatting | bytes 786432
Async XLA Ops:
  34.0 1.9 %copy-start.1 = (bf16[1,1,2,256,256]{4,3,2,1,0:T(8,128)(2,1)S(1)}, bf16[1,1,2,256,256]{4,3,2,1,0:T(8,128)(2,1)}, u32[]{:S(2)}) copy-start(bf16[1,1,2,256,256]{4,3,2,1,0:T(8,128)(2,1)} %get-tuple-element.7) | copy-start | bytes 786436
  36.0 1.1 %copy-start = (f32[1,256,384]{2,1,0:T(8,128)S(1)}, f32[1,256,384]{2,1,0:T(8,128)}, u32[]{:S(2)}) copy-start(f32[1,256,384]{2,1,0:T(8,128)} %get-tuple-element.8) | copy-start | bytes 1179652

commit v2 on v1

--- a/solution.py
+++ b/solution.py
@@ -13,9 +13,14 @@
 DEFOCUS = 6.0
 ROWS = 128
 STEP = 32
+VLIM = 55
 MESH = pl.DeviceIdType.MESH
 F32 = jnp.float32
 BF16 = jnp.bfloat16
+
+
+def rounded(x):
+    return x.real.astype(BF16).astype(np.float64) + 1j * x.imag.astype(BF16).astype(np.float64)
 
 
 def tables(n):
@@ -29,8 +34,19 @@
     f = cos_t - 1j * sin_t
     m = (np.conj(f) * q[None, :]) @ f
     m = (m + m.T) / 2
+    best = (np.inf, 1.0)
+    for size in np.linspace(0.7, 1.4, 64):
+        turns = size * np.exp(1j * np.linspace(0.0, math.pi / 2, 128, endpoint=False))
+        row = m[0][None, :] / turns[:, None]
+        miss = np.sum(np.abs(rounded(row) - row) ** 2, axis=1) * size * size
+        at = int(np.argmin(miss))
+        if miss[at] < best[0]:
+            best = (miss[at], turns[at])
+    z = best[1]
+    near = rounded(z * m)
+    rest = z * m - near
     g = np.conj(f) * q[None, :]
-    parts = (m.real, m.imag, cos_t, -sin_t, g.real, g.imag, g.T.real, g.T.imag)
+    parts = [x for v in (near, rest, m / z, f, g, g.T) for x in (v.real, v.imag)]
     return np.stack([p.astype(BF16) for p in parts])
 
 
@@ -59,11 +75,12 @@
 
 def kernel(
     sections, tiles,
-    pos, pot, probe, inten, fwd, adj, saved, tab,
+    pos, pot_h, probe_h, inten_h, fwd_h, adj_h, saved_h, tab_h,
     o_fwd, o_adj, o_grad,
-    in_f, in_b, out_f, out_b, l_f, r_f, l_b, r_b, l_g, r_g,
+    in_f, in_b, out_f, out_b, l_f, m_f, r_f, l_b, m_b, r_b, l_g, r_g,
     ext, tf, ta, bk, total, a_buf, y_buf,
     halo_out, halo_in, edge_out, edge_in,
+    pot, probe, inten, fwd, adj, saved, tab, load_sem,
     send_f, recv_f, send_b, recv_b, send_h, recv_h, send_e, recv_e,
 ):
     n = probe.shape[1]
@@ -76,6 +93,14 @@
     first, last = s == 0, s == sections - 1
     low, high = t == 0, t == tiles - 1
 
+    loads = {}
+    for i, (name, src, dst) in enumerate((
+        ("pot", pot_h, pot), ("tab", tab_h, tab), ("adj", adj_h, adj), ("fwd", fwd_h, fwd),
+        ("probe", probe_h, probe), ("saved", saved_h, saved), ("inten", inten_h, inten),
+    )):
+        loads[name] = pltpu.make_async_copy(src, dst, load_sem.at[i])
+        loads[name].start()
+
     barrier = pltpu.get_barrier_semaphore()
     one = lambda c: jnp.where(c, 1, 0).astype(jnp.int32)
 
@@ -88,6 +113,7 @@
     greet(s < sections - 1, "depth", s + 1)
     greet(t > 0, "tile", t - 1)
     greet(t < tiles - 1, "tile", t + 1)
+    loads["pot"].wait()
     halo_out[0] = pot[0, 0:margin, :].astype(BF16)
     halo_out[1] = pot[0, core - margin : core, :].astype(BF16)
     pl.semaphore_wait(barrier, one(s > 0) + one(s < sections - 1) + one(t > 0) + one(t < tiles - 1))
@@ -123,29 +149,41 @@
 
     tile_start(halo_out, halo_in, send_h, recv_h)
 
-    def fill(l_ref, r_ref, lr, li, rr, ri):
+    def fill_left(ref, lr, li):
         for c in range(nc):
             cols = slice(c * ROWS, (c + 1) * ROWS)
-            l_ref[c, 0:n, 0:ROWS] = lr[:, cols]
-            l_ref[c, 0:n, ROWS : 2 * ROWS] = -li[:, cols]
-            l_ref[c, n : 2 * n, 0:ROWS] = li[:, cols]
-            l_ref[c, n : 2 * n, ROWS : 2 * ROWS] = lr[:, cols]
-        r_ref[0:n, 0:n] = rr
-        r_ref[0:n, n : 2 * n] = ri
-        r_ref[n : 2 * n, 0:n] = -ri
-        r_ref[n : 2 * n, n : 2 * n] = rr
-
-    fill(l_b, r_b, tab[0], -tab[1], tab[0], -tab[1])
+            ref[c, 0:n, 0:ROWS] = lr[:, cols]
+            ref[c, 0:n, ROWS : 2 * ROWS] = -li[:, cols]
+            ref[c, n : 2 * n, 0:ROWS] = li[:, cols]
+            ref[c, n : 2 * n, ROWS : 2 * ROWS] = lr[:, cols]
+
+    def fill_right(ref, rr, ri):
+        ref[0:n, 0:n] = rr
+        ref[0:n, n : 2 * n] = ri
+        ref[n : 2 * n, 0:n] = -ri
+        ref[n : 2 * n, n : 2 * n] = rr
+
+    loads["tab"].wait()
+    fill_left(l_b, tab[0], -tab[1])
+    fill_left(m_b, tab[2], -tab[3])
+    fill_right(r_b, tab[4], -tab[5])
 
     @pl.when(jnp.logical_not(last))
     def _():
-        fill(l_f, r_f, tab[0], tab[1], tab[0], tab[1])
+        fill_left(l_f, tab[0], tab[1])
+        fill_left(m_f, tab[2], tab[3])
+        fill_right(r_f, tab[4], tab[5])
 
     @pl.when(last)
     def _():
-        fill(l_f, r_f, tab[2], tab[3], tab[2], tab[3])
-        fill(l_g, r_g, tab[4], tab[5], tab[6], tab[7])
-
+        fill_left(l_f, tab[6], tab[7])
+        m_f[...] = jnp.zeros_like(m_f)
+        fill_right(r_f, tab[6], tab[7])
+        fill_left(l_g, tab[8], tab[9])
+        fill_right(r_g, tab[10], tab[11])
+
+    for name in ("adj", "fwd", "probe"):
+        loads[name].wait()
     for c in range(nc):
         for part in range(2):
             rows = slice(c * ROWS, (c + 1) * ROWS)
@@ -186,8 +224,8 @@
         return jnp.where(ahead == offset, 1.0, 0.0).astype(BF16)
 
     def window(index, out):
-        rows = dot(chosen(pos[0, index, 0], 1), ext[...]).astype(BF16)
-        bk[0] = SIGMA * dot(rows, chosen(pos[0, index, 1], 0))
+        rows = dot(chosen(pos[0, 0, index], 1), ext[...]).astype(BF16)
+        bk[0] = SIGMA * dot(rows, chosen(pos[0, 1, index], 0))
         for at in range(0, n, STEP):
             sv, cv = sin_cos(bk[0, at : at + STEP, :])
             out[0, at : at + STEP, :] = cv
@@ -204,15 +242,13 @@
         more = slice(n + c * ROWS, n + (c + 1) * ROWS)
         return dot(jnp.concatenate([a_buf[rows, :], a_buf[more, :]], axis=1), r_ref[...])
 
-    def tick(k, carry):
-        window(k + s, ta)
-        window(k - s + 2 * sections - 1, tf)
+    def backward(k):
         acc = None
         for c in range(nc):
             @pl.when(jnp.logical_and(k > 0, jnp.logical_not(last)))
             def _():
                 copy_b(k - 1, c).wait_recv()
-            term = dot(l_b[c], in_b[k, c])
+            term = dot(l_b[c], in_b[k, c]) + dot(m_b[c], in_b[k, c])
             acc = term if acc is None else acc + term
         a_buf[...] = acc.astype(BF16)
         for c in range(nc):
@@ -230,6 +266,8 @@
             @pl.when(jnp.logical_not(first))
             def _():
                 copy_b(k, c).start()
+
+    def forward(k):
         acc = None
         for c in range(nc):
             rows = slice(c * ROWS, (c + 1) * ROWS)
@@ -241,7 +279,7 @@
             wi = in_f[k, c, ROWS : 2 * ROWS, :].astype(F32)
             tr, ti = tf[0, rows, :], tf[1, rows, :]
             u = jnp.concatenate([tr * wr - ti * wi, tr * wi + ti * wr], axis=0).astype(BF16)
-            term = dot(l_f[c], u)
+            term = dot(l_f[c], u) + dot(m_f[c], u)
             acc = term if acc is None else acc + term
         a_buf[...] = acc.astype(BF16)
 
@@ -272,16 +310,34 @@
                 in_b[k + 1, c, 0:ROWS, :] = out[:, 0:n].astype(BF16)
                 in_b[k + 1, c, ROWS : 2 * ROWS, :] = out[:, n : 2 * n].astype(BF16)
 
+    early = jnp.logical_or(first, jnp.logical_and(lax.rem(s, 2) == 1, jnp.logical_not(last)))
+
+    def tick(k, carry):
+        window(k + s, ta)
+        window(k - s + 2 * sections - 1, tf)
+
+        @pl.when(early)
+        def _():
+            forward(k)
+
+        backward(k)
+
+        @pl.when(jnp.logical_not(early))
+        def _():
+            forward(k)
+
         sr = saved[0, 0, k, 0].astype(F32)
         si = saved[0, 0, k, 1].astype(F32)
         delta = SIGMA * (bk[1] * sr - bk[0] * si)
         coarse = delta.astype(BF16)
         fine = (delta - coarse.astype(F32)).astype(BF16)
-        tall = dot(chosen(pos[0, k + s, 0], 0), jnp.concatenate([coarse, fine], axis=1)).astype(BF16)
-        across = chosen(pos[0, k + s, 1], 1)
+        tall = dot(chosen(pos[0, 0, k + s], 0), jnp.concatenate([coarse, fine], axis=1)).astype(BF16)
+        across = chosen(pos[0, 1, k + s], 1)
         total[...] += dot(tall[:, 0:n], across) + dot(tall[:, n : 2 * n], across)
         return carry
 
+    for name in ("saved", "inten"):
+        loads[name].wait()
     lax.fori_loop(0, ticks, tick, 0)
 
     edge_out[0] = total[0:margin, :].astype(BF16)
@@ -303,8 +359,8 @@
         @pl.when(jnp.logical_not(first))
         def _():
             copy_f(ticks - 1, c).wait_recv()
-        o_fwd[0, 0, 0, rows, :] = in_f[ticks, c, 0:ROWS, :].astype(F32)
-        o_fwd[0, 0, 1, rows, :] = in_f[ticks, c, ROWS : 2 * ROWS, :].astype(F32)
+        o_fwd[0, 0, 0, rows, :] = in_f[ticks, c, 0:ROWS, :]
+        o_fwd[0, 0, 1, rows, :] = in_f[ticks, c, ROWS : 2 * ROWS, :]
     for k in range(ticks):
         for c in range(nc):
             @pl.when(jnp.logical_not(last))
@@ -322,6 +378,8 @@
     ticks = intensity.shape[1]
     core, width = potential.shape[1], potential.shape[2]
     margin = (width - core) // 2
+    tab = jnp.asarray(tables(n))
+    held = lambda x: pltpu.VMEM(x.shape, x.dtype)
     vmem = pl.BlockSpec(memory_space=pltpu.VMEM)
     smem = pl.BlockSpec(memory_space=pltpu.SMEM)
     dma = lambda *shape: pltpu.SemaphoreType.DMA(shape)
@@ -330,31 +388,34 @@
     rt = pltpu.VMEM((2 * n, 2 * n), BF16)
     two = pltpu.VMEM((2, n, n), F32)
     strip = pltpu.VMEM((2, margin, width), BF16)
-    return pl.pallas_call(
+    wave_next, adj_next, gradient = pl.pallas_call(
         functools.partial(kernel, sections, tiles),
         out_shape=(
-            jax.ShapeDtypeStruct(fwd_wave.shape, F32),
+            jax.ShapeDtypeStruct(fwd_wave.shape, BF16),
             jax.ShapeDtypeStruct(adj_wave.shape, BF16),
             jax.ShapeDtypeStruct(potential.shape, F32),
         ),
-        in_specs=[smem] + [vmem] * 7,
+        in_specs=[smem] + [pl.BlockSpec(memory_space=pltpu.HBM)] * 7,
         out_specs=(vmem, vmem, vmem),
         scratch_shapes=[
             wave(ticks + 1), wave(ticks + 1), wave(ticks), wave(ticks),
-            lt, rt, lt, rt, lt, rt,
+            lt, lt, rt, lt, lt, rt, lt, rt,
             pltpu.VMEM((width, width), BF16), two, two, two,
             pltpu.VMEM((width, width), F32),
             pltpu.VMEM((2 * n, n), BF16),
             pltpu.VMEM((nc, 2 * ROWS, n), BF16),
             strip, strip, strip, strip,
+            held(potential), held(probe), held(intensity), held(fwd_wave), held(adj_wave),
+            held(saved_wave), held(tab), dma(7),
             dma(ticks, nc), dma(ticks, nc), dma(ticks, nc), dma(ticks, nc),
             dma(2), dma(2), dma(2), dma(2),
         ],
         compiler_params=pltpu.CompilerParams(
-            collective_id=0, has_side_effects=True, vmem_limit_bytes=60 * 1024 * 1024
+            collective_id=0, has_side_effects=True, vmem_limit_bytes=VLIM * 1024 * 1024
         ),
         name="window",
-    )(positions, potential, probe, intensity, fwd_wave, adj_wave, saved_wave, jnp.asarray(tables(n)))
+    )(jnp.swapaxes(positions, 1, 2), potential, probe, intensity, fwd_wave, adj_wave, saved_wave, tab)
+    return wave_next.astype(F32), adj_next, gradient
 
 
 def solution(mesh):

time: 38 us -> 35.2 us (0.926)
  local copies, waits for them, and re-layouts: 5.11 us -> 2.42 us
  Pallas kernels: 32 us -> 29.7 us
  other arithmetic: 0 us -> 1.83 us
    unnamed x8 -> x4, local copies, waits for them, and re-layouts: 5.11 us -> 2.42 us
    pallas_call x1, Pallas kernels: 32 us -> 29.7 us  [on_device(): pl.pallas_call(functools.partial(kernel, sections, tiles), out_shape=(jax...]
    convert_element_type x0 -> x1, other arithmetic: none -> 1.83 us  [on_device(): return (wave_next.astype(F32), adj_next, gradient)]
where the time goes in v2:
time: 35.2 us; the launch traced here: 34.6 us
  Pallas kernels  29.7 us (84%)
  local copies, waits for them, and re-layouts  2.42 us (7%)
  other arithmetic  1.83 us (5%)
  between operations  0.65 us (2%)
    pallas_call x1, Pallas kernels, on_device(): pl.pallas_call(functools.partial(kernel, sections, tiles), out_shape=(jax...  29.7 us
    unnamed x4, local copies, waits for them, and re-layouts  2.42 us
    convert_element_type x1, other arithmetic, on_device(): return (wave_next.astype(F32), adj_next, gradient)  1.83 us

profile of v2, /device:TPU:1, one launch (start us, length us, event | category | flops | bytes accessed | tf_op | source)
XLA Modules:
  0.0 34.6 jit_solution(12538695987463019887)
XLA Ops:
  0.6 29.7 %window.1 = (bf16[1,1,2,256,256]{4,3,2,1,0:T(8,128)(2,1)}, bf16[1,1,2,256,256]{4,3,2,1,0:T(8,128)(2,1)}, f32[1,256,384]{2,1,0:T(8,128)}) custom-call(s32[1,2,19]{2,1,0:T(2,128)} %bitcast.1, f32[1,256,384]{2,1,0:T(8,128)} %pot_h.1, bf16[2,256,256]{2,1,0:T(8,128)(2,1)} %probe_h.1, bf16[1,4,256,256]{3,2,1,0:T(8,128)(2,1)} %inten_h.1, ...), custom_call_target="tpu_custom_call" | custom-call | tf_op jit(solution)/shard_map/window/pallas_call | solution.py:391
  30.4 0.0 copy-start
  30.4 1.8 %convert_element_type.3 = f32[1,1,2,256,256]{4,3,2,1,0:T(8,128)} convert(bf16[1,1,2,256,256]{4,3,2,1,0:T(8,128)(2,1)} %get-tuple-element.6) | non-fusion elementwise | flops 131072 | bytes 786432 | tf_op jit(solution)/shard_map/convert_element_type | solution.py:418
  32.2 1.7 %copy.13 = bf16[1,1,2,256,256]{4,3,2,1,0:T(8,128)(2,1)} copy(bf16[1,1,2,256,256]{4,3,2,1,0:T(8,128)(2,1)} %get-tuple-element.13) | data formatting | bytes 524288
  33.9 0.0 copy-done
  33.9 0.7 %copy.14 = f32[1,256,384]{2,1,0:T(8,128)} copy(f32[1,256,384]{2,1,0:T(8,128)S(1)} %copy-done) | data formatting | bytes 786432
Async XLA Ops:
  30.4 3.5 %copy-start = (f32[1,256,384]{2,1,0:T(8,128)S(1)}, f32[1,256,384]{2,1,0:T(8,128)}, u32[]{:S(2)}) copy-start(f32[1,256,384]{2,1,0:T(8,128)} %get-tuple-element.14) | copy-start | bytes 1179652
